TPU v7x, 32 devices: a whole 2x2x4 slice. The times are simulated.
32 devices in a mesh: section: 4 (over y, x), tensor: 8 (over z, core).
Axes of the slice: x: 2, y: 2, z: 4, core: 2. Of those that a mesh axis runs over, the one named last changes fastest.
Arguments:
- tokens: bfloat16 [2, 32, 4096], P(None, 'tensor'), may hold values from -24 to 24
- expert_ids: int32 [4, 2, 32, 2], P('section', None, 'tensor'), may hold values from 0 to 7, as said below
- router_weight: bfloat16 [4, 4096, 8], P('section'), may hold values from -0.09375 to 0.09375
- norm_gain: float32 [4, 4096], P('section'), may hold values from 0.1 to 1.9
- gate_weight: bfloat16 [4, 28672, 4096], P('section', 'tensor'), may hold values from -0.09375 to 0.09375
- up_weight: bfloat16 [4, 28672, 4096], P('section', 'tensor'), may hold values from -0.09375 to 0.09375
- down_weight: bfloat16 [4, 28672, 4096], P('section', 'tensor'), may hold values from -0.046875 to 0.046875
Outputs:
- section_outputs: bfloat16 [4, 2, 32, 4096], P('section', None, 'tensor')
Inputs may be any that keep to these rules, and one draw needn't show every extreme that they name: `expert_ids`: each token names two different experts. Along the token dimension, in aligned blocks of 4 tokens of one micro-batch and one layer, at most 2 tokens name expert 0 and at most 2 name expert 1; in some micro-batch of every layer every block has exactly 2 of each.
All inputs are finite; a program needn't handle non-finite values.
Results may differ from a plain program's by a relative error of at most 0.0055.
Values may be sent and summed in bfloat16 or wider, within the bound.
A program may use at most 128 MiB of HBM per device.

v0:
```python
import jax
import jax.numpy as jnp
from jax import lax
from jax.sharding import PartitionSpec as P

EPSILON = 1e-05


def from_behind(block, axis, distance):
    devices = range(lax.axis_size(axis))
    route = [(i - distance, i) for i in devices if i - distance in devices]
    return lax.ppermute(block, axis, route)


def normalize(hidden_rows, gain):
    wide = hidden_rows.astype(jnp.float32)
    scale = lax.rsqrt(jnp.mean(wide * wide, axis=-1, keepdims=True) + EPSILON)
    return (wide * scale * gain).astype(jnp.bfloat16)


def mixing_weight(logits, routes, expert):
    routed = (routes[:, 0] == expert) | (routes[:, 1] == expert)
    partner = jnp.where(routes[:, 0] == expert, routes[:, 1], routes[:, 0])
    columns = lax.broadcasted_iota(jnp.int32, logits.shape, 1)
    partner_logit = jnp.sum(jnp.where(columns == partner[:, None], logits, 0.0), axis=1)
    value = 1.0 / (1.0 + jnp.exp(partner_logit - logits[:, expert]))
    return (jnp.where(routed, value, 0.0), routed.astype(jnp.int32))


def pickers(flags, slot_count):
    place = jnp.cumsum(flags, axis=1) - 1
    slots = lax.broadcasted_iota(jnp.int32, (1, slot_count, 1), 1)
    chosen = (place[:, None, :] == slots) & (flags[:, None, :] == 1)
    return chosen.astype(jnp.float32)


def project_rows(rows, weight_rows):
    return lax.dot_general(
        rows, weight_rows, (((1,), (1,)), ((), ())), preferred_element_type=jnp.float32
    )


def body(tokens, expert_ids, router_weight, norm_gain, gate_weight, up_weight, down_weight):
    sections = lax.axis_size("section")
    section = lax.axis_index("section")
    group = lax.axis_index("tensor") // (lax.axis_size("tensor") // 2)
    micro, count, width = tokens.shape
    slot_count = count // 2
    router = router_weight[0]
    gain = norm_gain[0]
    w_gate = gate_weight[0]
    w_up = up_weight[0]
    w_down = down_weight[0]
    all_routes = expert_ids[0]

    def expand(piece):
        gate = project_rows(piece, w_gate)
        upward = project_rows(piece, w_up)
        return (jax.nn.silu(gate) * upward).astype(jnp.bfloat16)

    def own_expert(piece):
        return expand(lax.dynamic_index_in_dim(piece, group, 0, keepdims=False))

    def layer(hidden_rows, routes):
        normed = normalize(hidden_rows, gain)
        logits = jnp.dot(normed, router, preferred_element_type=jnp.float32)
        weight_zero, flags_zero = mixing_weight(logits, routes, 0)
        weight_one, flags_one = mixing_weight(logits, routes, 1)
        pick_zero = pickers(flags_zero[None, :], slot_count)[0]
        pick_one = pickers(flags_one[None, :], slot_count)[0]
        both_picks = jnp.stack([pick_zero, pick_one]).astype(jnp.bfloat16)
        mine = jnp.einsum(
            "esj,jd->esd", both_picks, normed, preferred_element_type=jnp.float32
        ).astype(jnp.bfloat16)
        hidden = own_expert(lax.all_gather(mine, "tensor", axis=1, tiled=True))
        product = jnp.dot(hidden, w_down, preferred_element_type=jnp.float32)
        product = product.reshape(
            2 * slot_count * lax.axis_size("tensor") // (2 * slot_count), 1, slot_count, width
        )
        which = lax.broadcasted_iota(jnp.int32, (1, 2, 1, 1), 1)
        term = jnp.where(which == group, product, 0.0)
        summed = lax.psum_scatter(
            term.reshape(2 * slot_count * lax.axis_size("tensor"), width),
            "tensor",
            scatter_dimension=0,
            tiled=True,
        )
        expert_zero = jnp.dot(pick_zero.T, summed[:slot_count], precision=lax.Precision.HIGHEST)
        expert_one = jnp.dot(pick_one.T, summed[slot_count:], precision=lax.Precision.HIGHEST)
        total = (
            hidden_rows.astype(jnp.float32)
            + weight_zero[:, None] * expert_zero
            + weight_one[:, None] * expert_one
        )
        return total.astype(jnp.bfloat16)

    def advance(step, carry):
        incoming, stash = carry
        number = step - section
        active = (number >= 0) & (number < micro)
        position = jnp.clip(number, 0, micro - 1)
        fresh = lax.dynamic_index_in_dim(tokens, position, 0, keepdims=False)
        current = jnp.where(section == 0, fresh, incoming)
        routes = lax.dynamic_index_in_dim(all_routes, position, 0, keepdims=False)
        result = layer(current, routes)
        before = lax.dynamic_index_in_dim(stash, position, 0, keepdims=False)
        stash = lax.dynamic_update_index_in_dim(
            stash, jnp.where(active, result, before), position, 0
        )
        incoming = from_behind(result, "section", 1)
        return (incoming, stash)

    initial = (jnp.zeros((count, width), jnp.bfloat16), jnp.zeros_like(tokens))
    final_pass, stash = lax.fori_loop(0, micro + sections - 1, advance, initial)
    return stash[None]


def solution(mesh):
    return jax.shard_map(
        body,
        mesh=mesh,
        in_specs=(
            P(None, "tensor", None),
            P("section", None, "tensor", None),
            P("section", None, None),
            P("section", None),
            P("section", "tensor", None),
            P("section", "tensor", None),
            P("section", "tensor", None),
        ),
        out_specs=P("section", None, "tensor", None),
        check_vma=False,
    )
```

profile of v0, /device:TPU:7, one launch (start us, length us, event | category | flops | bytes accessed | tf_op | source)
XLA Modules:
  0.0 614.6 jit_solution(7769537876816631305)
XLA Ops:
  6.6 600.9 %while.18 = (s32[]{:T(128)}, bf16[4,4096]{1,0:T(4,128)(2,1)S(1)}, bf16[2,4,4096]{2,1,0:T(4,128)(2,1)S(1)}, pred[]{:T(512)}, s32[]{:T(128)}, /*index=5*/bf16[2,4,...) while((s32[]{:T(128)}, bf16[4,4096]{1,0:T(4,128)(2,1)S(1)}, ...), condition=%wide.region_7.8_spmd, body=%wide.region_0.7_spmd.sunk | while | flops 1411334528 | bytes 97111616 | solution.py:114
  11.6 14.9 %all_gather.12 = bf16[2,16,4096]{2,0,1:T(2,128)(2,1)S(1)} all-gather(bf16[2,2,4096]{2,0,1:T(2,128)(2,1)S(1)} %copy.47), channel_id=1, replica_groups=mesh['section'=4,'tensor'=8] {'tensor'}, dimensions={1}, use_global_device_ids=true | all-gather | bytes 294912 | tf_op jit(solution)/shard_map/while/body/eval_jaxpr/all_gather | solution.py:75
  26.9 13.2 %fusion.82 = f32[16,3584]{1,0:T(8,128)S(1)} fusion(bf16[3584,4096]{1,0:T(8,128)(2,1)} %get-tuple-element.569, bf16[1,16,4096]{2,0,1:T(2,128)(2,1)S(1)} %constant_dynamic-slice_fusion.6), kind=kOutput, calls=%fused_computation.22.clone.1 | convolution fusion | flops 469762048 | bytes 29720576 | tf_op jit(solution)/shard_map/while/body/eval_jaxpr/dot_general | solution.py:38
  40.1 21.8 %fusion.83 = f32[16,4096]{1,0:T(8,128)S(1)} fusion(bf16[3584,4096]{1,0:T(8,128)(2,1)} %get-tuple-element.571, bf16[3584,4096]{1,0:T(8,128)(2,1)} %get-tuple-element.570, f32[16,3584]{1,0:T(8,128)S(1)} %fusion.82, bf16[1,16,4096]{2,0,1:T(2,128)(2,1)S(1)} %constant_dynamic-slice_fusion.6), kind=kOutput, calls=%fused_computation.8.clone.1 | convolution fusion | flops 939868160 | bytes 59342848 | tf_op jit(solution)/shard_map/while/body/eval_jaxpr/dot_general | solution.py:76
  65.0 54.2 %all-reduce.5.cloned.1.call-done = f32[32,4096]{1,0:T(8,128)} async-done(((f32[32,4096]{1,0:T(8,128)}), f32[32,4096]{1,0:T(8,128)}) %all-reduce.5.cloned.1.call-update) | async-done | bytes 524304 | tf_op jit(solution)/shard_map/while
  123.0 3.4 collective-permute-done
  131.3 17.6 %all_gather.12 = bf16[2,16,4096]{2,0,1:T(2,128)(2,1)S(1)} all-gather(bf16[2,2,4096]{2,0,1:T(2,128)(2,1)S(1)} %copy.47), channel_id=1, replica_groups=mesh['section'=4,'tensor'=8] {'tensor'}, dimensions={1}, use_global_device_ids=true | all-gather | bytes 294912 | tf_op jit(solution)/shard_map/while/body/eval_jaxpr/all_gather | solution.py:75
  149.2 13.2 %fusion.82 = f32[16,3584]{1,0:T(8,128)S(1)} fusion(bf16[3584,4096]{1,0:T(8,128)(2,1)} %get-tuple-element.569, bf16[1,16,4096]{2,0,1:T(2,128)(2,1)S(1)} %constant_dynamic-slice_fusion.6), kind=kOutput, calls=%fused_computation.22.clone.1 | convolution fusion | flops 469762048 | bytes 29720576 | tf_op jit(solution)/shard_map/while/body/eval_jaxpr/dot_general | solution.py:38
  162.5 21.8 %fusion.83 = f32[16,4096]{1,0:T(8,128)S(1)} fusion(bf16[3584,4096]{1,0:T(8,128)(2,1)} %get-tuple-element.571, bf16[3584,4096]{1,0:T(8,128)(2,1)} %get-tuple-element.570, f32[16,3584]{1,0:T(8,128)S(1)} %fusion.82, bf16[1,16,4096]{2,0,1:T(2,128)(2,1)S(1)} %constant_dynamic-slice_fusion.6), kind=kOutput, calls=%fused_computation.8.clone.1 | convolution fusion | flops 939868160 | bytes 59342848 | tf_op jit(solution)/shard_map/while/body/eval_jaxpr/dot_general | solution.py:76
  187.4 52.2 %all-reduce.5.cloned.1.call-done = f32[32,4096]{1,0:T(8,128)} async-done(((f32[32,4096]{1,0:T(8,128)}), f32[32,4096]{1,0:T(8,128)}) %all-reduce.5.cloned.1.call-update) | async-done | bytes 524304 | tf_op jit(solution)/shard_map/while
  243.2 3.4 collective-permute-done
  251.6 17.6 %all_gather.12 = bf16[2,16,4096]{2,0,1:T(2,128)(2,1)S(1)} all-gather(bf16[2,2,4096]{2,0,1:T(2,128)(2,1)S(1)} %copy.47), channel_id=1, replica_groups=mesh['section'=4,'tensor'=8] {'tensor'}, dimensions={1}, use_global_device_ids=true | all-gather | bytes 294912 | tf_op jit(solution)/shard_map/while/body/eval_jaxpr/all_gather | solution.py:75
  269.5 13.2 %fusion.82 = f32[16,3584]{1,0:T(8,128)S(1)} fusion(bf16[3584,4096]{1,0:T(8,128)(2,1)} %get-tuple-element.569, bf16[1,16,4096]{2,0,1:T(2,128)(2,1)S(1)} %constant_dynamic-slice_fusion.6), kind=kOutput, calls=%fused_computation.22.clone.1 | convolution fusion | flops 469762048 | bytes 29720576 | tf_op jit(solution)/shard_map/while/body/eval_jaxpr/dot_general | solution.py:38
  282.8 21.8 %fusion.83 = f32[16,4096]{1,0:T(8,128)S(1)} fusion(bf16[3584,4096]{1,0:T(8,128)(2,1)} %get-tuple-element.571, bf16[3584,4096]{1,0:T(8,128)(2,1)} %get-tuple-element.570, f32[16,3584]{1,0:T(8,128)S(1)} %fusion.82, bf16[1,16,4096]{2,0,1:T(2,128)(2,1)S(1)} %constant_dynamic-slice_fusion.6), kind=kOutput, calls=%fused_computation.8.clone.1 | convolution fusion | flops 939868160 | bytes 59342848 | tf_op jit(solution)/shard_map/while/body/eval_jaxpr/dot_general | solution.py:76
  307.7 52.2 %all-reduce.5.cloned.1.call-done = f32[32,4096]{1,0:T(8,128)} async-done(((f32[32,4096]{1,0:T(8,128)}), f32[32,4096]{1,0:T(8,128)}) %all-reduce.5.cloned.1.call-update) | async-done | bytes 524304 | tf_op jit(solution)/shard_map/while
  363.5 3.4 collective-permute-done
  371.9 17.6 %all_gather.12 = bf16[2,16,4096]{2,0,1:T(2,128)(2,1)S(1)} all-gather(bf16[2,2,4096]{2,0,1:T(2,128)(2,1)S(1)} %copy.47), channel_id=1, replica_groups=mesh['section'=4,'tensor'=8] {'tensor'}, dimensions={1}, use_global_device_ids=true | all-gather | bytes 294912 | tf_op jit(solution)/shard_map/while/body/eval_jaxpr/all_gather | solution.py:75
  389.8 13.2 %fusion.82 = f32[16,3584]{1,0:T(8,128)S(1)} fusion(bf16[3584,4096]{1,0:T(8,128)(2,1)} %get-tuple-element.569, bf16[1,16,4096]{2,0,1:T(2,128)(2,1)S(1)} %constant_dynamic-slice_fusion.6), kind=kOutput, calls=%fused_computation.22.clone.1 | convolution fusion | flops 469762048 | bytes 29720576 | tf_op jit(solution)/shard_map/while/body/eval_jaxpr/dot_general | solution.py:38
  403.1 21.8 %fusion.83 = f32[16,4096]{1,0:T(8,128)S(1)} fusion(bf16[3584,4096]{1,0:T(8,128)(2,1)} %get-tuple-element.571, bf16[3584,4096]{1,0:T(8,128)(2,1)} %get-tuple-element.570, f32[16,3584]{1,0:T(8,128)S(1)} %fusion.82, bf16[1,16,4096]{2,0,1:T(2,128)(2,1)S(1)} %constant_dynamic-slice_fusion.6), kind=kOutput, calls=%fused_computation.8.clone.1 | convolution fusion | flops 939868160 | bytes 59342848 | tf_op jit(solution)/shard_map/while/body/eval_jaxpr/dot_general | solution.py:76
  427.9 52.2 %all-reduce.5.cloned.1.call-done = f32[32,4096]{1,0:T(8,128)} async-done(((f32[32,4096]{1,0:T(8,128)}), f32[32,4096]{1,0:T(8,128)}) %all-reduce.5.cloned.1.call-update) | async-done | bytes 524304 | tf_op jit(solution)/shard_map/while
  492.2 17.6 %all_gather.12 = bf16[2,16,4096]{2,0,1:T(2,128)(2,1)S(1)} all-gather(bf16[2,2,4096]{2,0,1:T(2,128)(2,1)S(1)} %copy.47), channel_id=1, replica_groups=mesh['section'=4,'tensor'=8] {'tensor'}, dimensions={1}, use_global_device_ids=true | all-gather | bytes 294912 | tf_op jit(solution)/shard_map/while/body/eval_jaxpr/all_gather | solution.py:75
  510.1 13.2 %fusion.82 = f32[16,3584]{1,0:T(8,128)S(1)} fusion(bf16[3584,4096]{1,0:T(8,128)(2,1)} %get-tuple-element.569, bf16[1,16,4096]{2,0,1:T(2,128)(2,1)S(1)} %constant_dynamic-slice_fusion.6), kind=kOutput, calls=%fused_computation.22.clone.1 | convolution fusion | flops 469762048 | bytes 29720576 | tf_op jit(solution)/shard_map/while/body/eval_jaxpr/dot_general | solution.py:38
  523.4 21.8 %fusion.83 = f32[16,4096]{1,0:T(8,128)S(1)} fusion(bf16[3584,4096]{1,0:T(8,128)(2,1)} %get-tuple-element.571, bf16[3584,4096]{1,0:T(8,128)(2,1)} %get-tuple-element.570, f32[16,3584]{1,0:T(8,128)S(1)} %fusion.82, bf16[1,16,4096]{2,0,1:T(2,128)(2,1)S(1)} %constant_dynamic-slice_fusion.6), kind=kOutput, calls=%fused_computation.8.clone.1 | convolution fusion | flops 939868160 | bytes 59342848 | tf_op jit(solution)/shard_map/while/body/eval_jaxpr/dot_general | solution.py:76
  548.2 52.2 %all-reduce.5.cloned.1.call-done = f32[32,4096]{1,0:T(8,128)} async-done(((f32[32,4096]{1,0:T(8,128)}), f32[32,4096]{1,0:T(8,128)}) %all-reduce.5.cloned.1.call-update) | async-done | bytes 524304 | tf_op jit(solution)/shard_map/while
  (196 shorter events, 64.2 us)
Async XLA Ops:
  6.6 112.6 %all-reduce.5.cloned.1.call-start = ((), (), s32[]{:S(2)}) async-start(), calls=%async_computation | async-start | bytes 1048576 | tf_op jit(solution)/shard_map/while
  40.1 23.7 %copy-start.1 = (u32[32]{0:T(128)S(1)}, u32[32]{0:T(128)}, u32[]{:S(2)}) copy-start(u32[32]{0:T(128)} %get-tuple-element.575) | copy-start | bytes 388 | tf_op jit(solution)/shard_map/while
  121.6 4.7 collective-permute-start
  126.3 113.2 %all-reduce.5.cloned.1.call-start = ((), (), s32[]{:S(2)}) async-start(), calls=%async_computation | async-start | bytes 1048576 | tf_op jit(solution)/shard_map/while
  162.5 23.7 %copy-start.1 = (u32[32]{0:T(128)S(1)}, u32[32]{0:T(128)}, u32[]{:S(2)}) copy-start(u32[32]{0:T(128)} %get-tuple-element.575) | copy-start | bytes 388 | tf_op jit(solution)/shard_map/while
  241.9 4.7 collective-permute-start
  246.6 113.2 %all-reduce.5.cloned.1.call-start = ((), (), s32[]{:S(2)}) async-start(), calls=%async_computation | async-start | bytes 1048576 | tf_op jit(solution)/shard_map/while
  282.8 23.7 %copy-start.1 = (u32[32]{0:T(128)S(1)}, u32[32]{0:T(128)}, u32[]{:S(2)}) copy-start(u32[32]{0:T(128)} %get-tuple-element.575) | copy-start | bytes 388 | tf_op jit(solution)/shard_map/while
  362.2 4.7 collective-permute-start
  366.9 113.2 %all-reduce.5.cloned.1.call-start = ((), (), s32[]{:S(2)}) async-start(), calls=%async_computation | async-start | bytes 1048576 | tf_op jit(solution)/shard_map/while
  403.1 23.7 %copy-start.1 = (u32[32]{0:T(128)S(1)}, u32[32]{0:T(128)}, u32[]{:S(2)}) copy-start(u32[32]{0:T(128)} %get-tuple-element.575) | copy-start | bytes 388 | tf_op jit(solution)/shard_map/while
  482.5 4.7 collective-permute-start
  487.2 113.2 %all-reduce.5.cloned.1.call-start = ((), (), s32[]{:S(2)}) async-start(), calls=%async_computation | async-start | bytes 1048576 | tf_op jit(solution)/shard_map/while
  523.3 23.7 %copy-start.1 = (u32[32]{0:T(128)S(1)}, u32[32]{0:T(128)}, u32[]{:S(2)}) copy-start(u32[32]{0:T(128)} %get-tuple-element.575) | copy-start | bytes 388 | tf_op jit(solution)/shard_map/while
  602.8 4.7 collective-permute-start
  607.5 0.6 copy-start
Sparse Core Ops, SparseCore 0:
  64.0 55.2 all-reduce.4
  186.3 53.1 all-reduce.4
  306.6 53.1 all-reduce.4
  426.9 53.1 all-reduce.4
  547.2 53.1 all-reduce.4
where the time goes:
time: 620 us; the launch traced here: 615 us
  waiting for transfers between devices  280 us (45%)
  matrix products  194 us (31%)
  blocking collectives  85.4 us (14%)
  other arithmetic  17.4 us (3%)
  local copies, waits for them, and re-layouts  15.1 us (2%)
  between operations  13.1 us (2%)
  starting transfers between devices  6.51 us (1%)
    while x10, waiting for transfers between devices  263 us
    dot_general x5, matrix products, layer(): product = jnp.dot(hidden, w_down, preferred_element_type=jnp.float32)  109 us
    all_gather x5, blocking collectives, layer(): hidden = own_expert(lax.all_gather(mine, 'tensor', axis=1, tiled=True))  85.4 us
    dot_general x5, matrix products, project_rows(): lax.dot_general(rows, weight_rows, (((1,), (1,)), ((), ())), preferred_el...  66.2 us
    ppermute x5, waiting for transfers between devices, from_behind(): return lax.ppermute(block, axis, route)  16.8 us
  transfers between devices with their start and end apart: 10, of which 10 were waited for; matrix products, arithmetic and copies ran while one was open for 0% of the time, Pallas kernels for 0%

commit v1 on v0

v1 whole, which is shorter than its diff:
```python
import functools

import jax
import jax.numpy as jnp
from jax import lax
from jax.experimental import pallas as pl
from jax.experimental.pallas import tpu as pltpu
from jax.sharding import PartitionSpec as P

EPSILON = 1e-05
PARTS = 4
MESH = pl.DeviceIdType.MESH


def kernel(
    n, sections, chunk, pairs, extra,
    ids, tokens, router, gain, w_gate, w_up, w_down, out,
    pool, h_in, h_out, mine, gathered, x, hidden, back, returned,
    gate_sem, down_sem, send_sem, recv_sem, back_sem, ret_sem, hop_send, hop_recv,
):
    section = lax.axis_index("section")
    me = lax.axis_index("tensor")
    half = n // 2
    group = me // half
    micro, count, width = tokens.shape
    slots = count // 2
    rows = micro * count
    packed = micro * slots
    part = width // PARTS
    total_slots = 2 * pairs + extra

    def weight_copy(source, j, which):
        place = 2 * j + which
        start = pl.multiple_of(j * chunk, chunk)
        return pltpu.make_async_copy(
            source.at[0, pl.ds(start, chunk), :], pool.at[place], gate_sem.at[place]
        )

    def down_place(block):
        return lax.rem(2 * pairs + block // PARTS, total_slots), block % PARTS

    def down_copy(block):
        place, column = down_place(block)
        row = pl.multiple_of((block % pairs) * chunk, chunk)
        source_column = pl.multiple_of((block // pairs) * part, part)
        column = pl.multiple_of(column * part, part)
        return pltpu.make_async_copy(
            w_down.at[0, pl.ds(row, chunk), pl.ds(source_column, part)],
            pool.at[place, :, pl.ds(column, part)],
            down_sem.at[block],
        )

    @pl.loop(0, pairs)
    def _(j):
        weight_copy(w_gate, j, 0).start()
        weight_copy(w_up, j, 1).start()

    for block in range(extra * PARTS):
        down_copy(block).start()

    barrier = pltpu.get_barrier_semaphore()

    @pl.loop(1, n)
    def _(k):
        pl.semaphore_signal(
            barrier, inc=1, device_id={"tensor": lax.rem(me + k, n)}, device_id_type=MESH
        )

    after = lax.rem(section + 1, sections)
    before = lax.rem(section + sections - 1, sections)
    for other in (after, before):
        pl.semaphore_signal(barrier, inc=1, device_id={"section": other}, device_id_type=MESH)
    pl.semaphore_wait(barrier, n + 1)

    row8 = lax.broadcasted_iota(jnp.int32, (rows, 128), 0)
    lane8 = lax.broadcasted_iota(jnp.int32, (rows, 128), 1)
    row_p = lax.broadcasted_iota(jnp.int32, (2 * packed, 128), 0)
    lane_p = lax.broadcasted_iota(jnp.int32, (2 * packed, 128), 1)
    pick = jnp.zeros((2 * packed, 128), jnp.float32)
    pick_t = jnp.zeros((rows, 128), jnp.float32)
    signs = []
    for expert in range(2):
        sign = jnp.zeros((rows, 128), jnp.float32)
        for m in range(micro):
            used = jnp.int32(0)
            for t in range(count):
                first = ids[0, m, t, 0]
                second = ids[0, m, t, 1]
                routed = (first == expert) | (second == expert)
                partner = jnp.where(first == expert, second, first)
                slot = expert * packed + m * slots + used
                slot = jnp.where(routed, slot, -1)
                used = used + routed.astype(jnp.int32)
                token = m * count + t
                pick = jnp.where((row_p == slot) & (lane_p == token), 1.0, pick)
                pick_t = jnp.where((row8 == token) & (lane8 == slot), 1.0, pick_t)
                sign = jnp.where((row8 == token) & (lane8 == partner), 1.0, sign)
        signs.append(sign - (lane8 == expert).astype(jnp.float32))

    hop = pltpu.make_async_remote_copy(
        src_ref=h_out, dst_ref=h_in, send_sem=hop_send, recv_sem=hop_recv,
        device_id={"section": after}, device_id_type=MESH,
    )

    @pl.when(section == 0)
    def _():
        h_in[...] = tokens[...]

    @pl.when(section > 0)
    def _():
        hop.wait_recv()

    h = jnp.concatenate([h_in[m].astype(jnp.float32) for m in range(micro)], axis=0)
    scale = lax.rsqrt(jnp.mean(h * h, axis=-1, keepdims=True) + EPSILON)
    normed = (h * scale * gain[...]).astype(jnp.bfloat16).astype(jnp.float32)
    chosen = pick[:, 0:1] * normed[0:1, :]
    for t in range(1, rows):
        chosen = chosen + pick[:, t : t + 1] * normed[t : t + 1, :]
    for expert in range(2):
        mine[expert] = chosen[expert * packed : (expert + 1) * packed].astype(jnp.bfloat16)

    def dispatch(peer):
        return pltpu.make_async_remote_copy(
            src_ref=mine.at[peer // half], dst_ref=gathered.at[me],
            send_sem=send_sem.at[peer], recv_sem=recv_sem.at[me],
            device_id={"tensor": peer}, device_id_type=MESH,
        )

    def arrival(peer):
        return pltpu.make_async_copy(mine.at[0], gathered.at[peer], recv_sem.at[peer])

    @pl.loop(1, n)
    def _(k):
        dispatch(lax.rem(me + k, n)).start()

    gathered[me] = mine[group]

    wide = jnp.concatenate([normed, normed], axis=0).astype(jnp.bfloat16)
    logits = jnp.dot(wide, router[0], preferred_element_type=jnp.float32)[:rows]
    experts = logits.shape[1]
    weights = []
    for expert in range(2):
        gap = jnp.sum(signs[expert][:, :experts] * logits, axis=1, keepdims=True)
        weights.append(1.0 / (1.0 + jnp.exp(gap)))
    coefficient = pick_t * jnp.where(lane8 < packed, weights[0], weights[1])

    @pl.loop(1, n)
    def _(k):
        arrival(lax.rem(me + k, n)).wait()

    step = 8 // packed
    for i in range(0, n, 2 * step):
        block = [gathered[i + a].astype(jnp.float32) for a in range(2 * step)]
        x[i * packed : (i + 2 * step) * packed, :] = jnp.concatenate(block, axis=0).astype(
            jnp.bfloat16
        )

    def project(place):
        return lax.dot_general(
            x[...], pool[place], (((1,), (1,)), ((), ())), preferred_element_type=jnp.float32
        )

    @pl.loop(0, pairs)
    def _(j):
        weight_copy(w_gate, j, 0).wait()
        gate = project(2 * j)
        weight_copy(w_up, j, 1).wait()
        upward = project(2 * j + 1)
        hidden[j] = (gate / (1.0 + jnp.exp(-gate)) * upward).astype(jnp.bfloat16)
        for a in range(2):
            late = 2 * j + extra + a

            @pl.when(late < pairs)
            def _():
                for b in range(PARTS):
                    down_copy(late * PARTS + b).start()

    def give_back(q, peer):
        return pltpu.make_async_remote_copy(
            src_ref=back.at[peer, q], dst_ref=returned.at[me, q],
            send_sem=back_sem.at[peer], recv_sem=ret_sem.at[me],
            device_id={"tensor": peer}, device_id_type=MESH,
        )

    for q in range(PARTS):
        for i in range(pairs):
            down_copy(q * pairs + i).wait()
        total = None
        for i in range(pairs):
            block = q * pairs + i
            place = (2 * pairs + block // PARTS) % total_slots
            column = (block % PARTS) * part
            term = jnp.dot(
                hidden[i], pool[place, :, column : column + part],
                preferred_element_type=jnp.float32,
            )
            total = term if total is None else total + term
        for i in range(n):
            back[i, q] = total[i * packed : (i + 1) * packed].astype(jnp.bfloat16)

        @pl.loop(1, n)
        def _(k):
            give_back(q, lax.rem(me + k, n)).start()

    returned[me] = back[me]

    @pl.loop(1, n)
    def _(k):
        peer = lax.rem(me + k, n)
        pltpu.make_async_copy(back.at[peer], returned.at[peer], ret_sem.at[peer]).wait()

    for q in range(PARTS):
        columns = slice(q * part, (q + 1) * part)
        sums = []
        for expert in range(2):
            value = returned[expert * half, q].astype(jnp.float32)
            for i in range(1, half):
                value = value + returned[expert * half + i, q].astype(jnp.float32)
            sums.append(value)
        result = jnp.concatenate([h_in[m, :, columns].astype(jnp.float32) for m in range(micro)], axis=0)
        for expert in range(2):
            for r in range(packed):
                slot = expert * packed + r
                result = result + coefficient[:, slot : slot + 1] * sums[expert][r : r + 1, :]
        for m in range(micro):
            h_out[m, :, columns] = result[m * count : (m + 1) * count].astype(jnp.bfloat16)

    @pl.when(section < sections - 1)
    def _():
        hop.start()

    out[0] = h_out[...]

    @pl.when(section < sections - 1)
    def _():
        hop.wait_send()

    @pl.loop(1, n)
    def _(k):
        peer = lax.rem(me + k, n)
        dispatch(peer).wait_send()
        pltpu.make_async_copy(back.at[peer], returned.at[peer], back_sem.at[peer]).wait()


def body(tokens, expert_ids, router_weight, norm_gain, gate_weight, up_weight, down_weight):
    n = lax.axis_size("tensor")
    sections = lax.axis_size("section")
    micro, count, width = tokens.shape
    packed = micro * count // 2
    held = gate_weight.shape[1]
    chunk = 256 if held % 256 == 0 else held
    pairs = held // chunk
    extra = min(2, pairs)
    bf16 = jnp.bfloat16
    vmem = pl.BlockSpec(memory_space=pltpu.VMEM)
    hbm = pl.BlockSpec(memory_space=pl.ANY)
    dma = pltpu.SemaphoreType.DMA
    return pl.pallas_call(
        functools.partial(kernel, n, sections, chunk, pairs, extra),
        out_shape=jax.ShapeDtypeStruct((1, micro, count, width), bf16),
        in_specs=[pl.BlockSpec(memory_space=pltpu.SMEM), vmem, vmem, vmem, hbm, hbm, hbm],
        out_specs=vmem,
        scratch_shapes=[
            pltpu.VMEM((2 * pairs + extra, chunk, width), bf16),
            pltpu.VMEM((micro, count, width), bf16),
            pltpu.VMEM((micro, count, width), bf16),
            pltpu.VMEM((2, packed, width), bf16),
            pltpu.VMEM((n, packed, width), bf16),
            pltpu.VMEM((n * packed, width), bf16),
            pltpu.VMEM((pairs, n * packed, chunk), bf16),
            pltpu.VMEM((n, PARTS, packed, width // PARTS), bf16),
            pltpu.VMEM((n, PARTS, packed, width // PARTS), bf16),
            dma((2 * pairs,)),
            dma((PARTS * pairs,)),
            dma((n,)),
            dma((n,)),
            dma((n,)),
            dma((n,)),
            dma,
            dma,
        ],
        compiler_params=pltpu.CompilerParams(
            collective_id=0, has_side_effects=True, vmem_limit_bytes=67043328
        ),
    )(expert_ids, tokens, router_weight, norm_gain, gate_weight, up_weight, down_weight)


def solution(mesh):
    return jax.shard_map(
        body,
        mesh=mesh,
        in_specs=(
            P(None, "tensor", None),
            P("section", None, "tensor", None),
            P("section", None, None),
            P("section", None),
            P("section", "tensor", None),
            P("section", "tensor", None),
            P("section", "tensor", None),
        ),
        out_specs=P("section", None, "tensor", None),
        check_vma=False,
    )
```

time: 620 us -> 225 us (0.36)
  waiting for transfers between devices: 280 us -> 0 us
  Pallas kernels: 0 us -> 220 us
  matrix products: 194 us -> 0 us
  blocking collectives: 85.4 us -> 0 us
  other arithmetic: 17.4 us -> 0 us
  between operations: 13.1 us -> 0.01 us
  local copies, waits for them, and re-layouts: 15.1 us -> 5.02 us
  starting transfers between devices: 6.51 us -> 0 us
    while x10 -> x0, waiting for transfers between devices: 263 us -> none
    pallas_call x0 -> x1, Pallas kernels: none -> 220 us  [body(): pl.pallas_call(functools.partial(kernel, n, sections, chunk, pairs, extra...]
    dot_general x30 -> x0, matrix products: 194 us -> none  [the longest x5 109 us: layer(): product = jnp.dot(hidden, w_down, preferred_element_type=jnp.float32)]
    all_gather x5 -> x0, blocking collectives: 85.4 us -> none  [layer(): hidden = own_expert(lax.all_gather(mine, 'tensor', axis=1, tiled=True))]
    ppermute x5 -> x0, waiting for transfers between devices: 16.8 us -> none  [from_behind(): return lax.ppermute(block, axis, route)]
    ppermute x5 -> x0, starting transfers between devices: 6.46 us -> none  [from_behind(): return lax.ppermute(block, axis, route)]
    select_n x15 -> x0, other arithmetic: 6.33 us -> none  [the longest x5 4.61 us: layer(): term = jnp.where(which == group, product, 0.0)]
  transfers between devices with their start and end apart: 10 -> 0, of which waited for: 10 -> 0; matrix products, arithmetic and copies ran while one was open for 0% -> 0% of each run, Pallas kernels for 0% -> 0%
where the time goes in v1:
time: 225 us
  Pallas kernels  220 us (98%)
  local copies, waits for them, and re-layouts  5.02 us (2%)
    pallas_call x1, Pallas kernels, body(): pl.pallas_call(functools.partial(kernel, n, sections, chunk, pairs, extra...  220 us
    unnamed x3, local copies, waits for them, and re-layouts  5.02 us

profile of v1, /device:TPU:7, one launch (start us, length us, event | category | flops | bytes accessed | tf_op | source)
XLA Modules:
  0.0 224.7 jit_solution(3346374811703191084)
XLA Ops:
  0.0 1.4 copy.8.ids
  1.4 2.2 copy.9.router
  3.5 219.7 %shard_map.73 = bf16[1,2,4,4096]{3,2,1,0:T(4,128)(2,1)} custom-call(s32[1,2,4,2]{3,2,1,0:T(4,128)} %copy.8.ids, bf16[2,4,4096]{2,1,0:T(4,128)(2,1)} %tokens.1, bf16[1,4096,8]{2,1,0:T(8,128)(2,1)} %copy.9.router, f32[1,4096]{1,0:T(1,128)} %gain.1, bf16[1,3584,4096]{2,1,0:T(8,128)(2,1)} %w_gate.1, bf16[1,3584,4096]{2,1,0:T(8,128)(2,1)} %w_up.1, ...), custom_call_target="tpu_custom_call" | custom-call | tf_op jit(solution)/shard_map/pallas_call | solution.py:258
  223.2 1.5 copy.11
